TPU v7x, 32 devices: a whole 2x2x4 slice. The times are simulated.
32 devices in a mesh: groups: 2 (over y), lon: 16 (over z, x, core).
Axes of the slice: x: 2, y: 2, z: 4, core: 2. Of those that a mesh axis runs over, the one named last changes fastest.
Arguments:
- fields: bfloat16 [4, 24, 192, 192], P('groups', None, 'lon'), parts along dimension 0, may hold values from -6 to 6
- norm_gain: float32 [192], replicated, may hold values from 0.25 to 1.75
- qkv_weight: bfloat16 [192, 576], replicated, may hold values from -2.5 to 2.5
- proj_weight: bfloat16 [192, 192], replicated, may hold values from -0.4375 to 0.4375
- bias_table: float32 [4, 6, 3312], replicated, may hold values from -4 to 4
- bias_index: int32 [144, 144], replicated, may hold values from 0 to 3311
- region_ids: int32 [2, 24], replicated, may hold values from 0 to 2
- mlp_gain: float32 [192], replicated, may hold values from 0.25 to 1.75
- up_weight: bfloat16 [192, 768], replicated, may hold values from -0.4375 to 0.4375
- down_weight: bfloat16 [768, 192], replicated, may hold values from -0.21875 to 0.21875
- merge_gain: float32 [768], replicated, may hold values from 0.25 to 1.75
- merge_weight: bfloat16 [768, 384], replicated, may hold values from -0.21875 to 0.21875
- cotangent: bfloat16 [4, 12, 96, 384], P('groups', None, 'lon'), parts along dimension 0, may hold values from -12 to 12
Outputs:
- merged: bfloat16 [4, 12, 96, 384], P('groups', None, 'lon'), parts along dimension 0
- field_grad: bfloat16 [4, 24, 192, 192], P('groups', None, 'lon'), parts along dimension 0
- qkv_grad: float32 [384, 576], P('groups'), parts along dimension 0
- proj_grad: float32 [384, 192], P('groups'), parts along dimension 0
- up_grad: float32 [384, 768], P('groups'), parts along dimension 0
- down_grad: float32 [1536, 192], P('groups'), parts along dimension 0
- merge_grad: float32 [1536, 384], P('groups'), parts along dimension 0
- table_grad: float32 [8, 6, 3312], P('groups'), parts along dimension 0
There are 2 independent parts, one for each index of `groups`. A program takes and returns all parts, laid end to end along the dimension named above; an argument that names none is the same for every part. Nothing has to cross between parts.
All inputs are finite; a program needn't handle non-finite values.
Results may differ from a plain program's by a relative error of at most 0.019.
The roundings to bfloat16 on the way count: a program that leaves them out, or rounds other values in their place, can miss the bound.
Values may be sent and summed in bfloat16 or wider, within the bound.
A program may use at most 192 MiB of HBM per device.

v0:
```python
import functools

import jax
import jax.numpy as jnp
import numpy as np
from jax import lax
from jax.experimental import pallas as pl
from jax.experimental.pallas import tpu as pltpu
from jax.sharding import PartitionSpec as P

C = 192
MLP = 768
HEADS = 6
HEAD = 32
WZ = 2
WLAT = 6
WLON = 12
HALF = 6
WIN = 144
BPOS = 3312
Z = 2
LAT = 24
TYPES = 4
TH = TYPES * HEADS
LANES = 128
KEYS = 256
RADIX = 256
DIGITS = -(-BPOS // RADIX)
GROUP = WIN // 4
GPAD = 48
ROWS_W = 30 * C
ROWS_T = DIGITS * TH * 2
BF = jnp.bfloat16
F32 = jnp.float32
VMEM = pl.BlockSpec(memory_space=pltpu.VMEM)


def dot(a, b, dims=((1,), (0,))):
    return lax.dot_general(a, b, (dims, ((), ())), preferred_element_type=F32)


NT = ((1,), (1,))
TN = ((0,), (0,))


def bias_kernel(high_ref, low_ref, digit_ref, lane_ref, out_ref):
    def row(i, carry):
        lane = lane_ref[pl.ds(i, 1), :]
        digit = digit_ref[pl.ds(i, 1), :]
        hot = (lax.broadcasted_iota(jnp.int32, (RADIX, KEYS), 0) == lane).astype(BF)
        high = dot(high_ref[...], hot)
        low = dot(low_ref[...], hot)
        total = jnp.zeros((TH, KEYS), F32)
        for d in range(DIGITS):
            piece = high[d * TH:(d + 1) * TH] + low[d * TH:(d + 1) * TH]
            total = jnp.where(digit == d, piece, total)
        rows = pl.ds(pl.multiple_of(i * TH, TH), TH)
        out_ref[0, rows, :] = total[:, :LANES]
        out_ref[1, rows, :] = total[:, LANES:]
        return carry

    lax.fori_loop(0, WIN, row, 0)


def norm_parts(values):
    average = jnp.mean(values, axis=-1, keepdims=True)
    centred = values - average
    variance = jnp.mean(centred * centred, axis=-1, keepdims=True)
    scale = lax.rsqrt(variance + 1e-05)
    return centred * scale, scale


def norm_grad(hat, scale, grad_hat):
    first = jnp.mean(grad_hat, axis=-1, keepdims=True)
    second = jnp.mean(grad_hat * hat, axis=-1, keepdims=True)
    return scale * (grad_hat - first - hat * second)


def block_kernel(
    x_ref, ct_ref, bias_ref, regq_ref, regk_ref, digit_ref, lane_ref, perm_ref,
    g1_ref, wqkv_ref, wproj_ref, g2_ref, wup_ref, wdown_ref, gm_ref, wm_ref,
    merged_ref, fgrad_ref, packed_ref,
    triple, prob, mixed, dmixed, dtriple, dscore,
    s_normed, s_dtriple, s_mixed, s_da, s_nmlp, s_du, s_hidden, s_dy, s_merge, s_table,
):
    s_merge[...] = jnp.zeros_like(s_merge)
    triple[...] = jnp.zeros_like(triple)
    root = float(HEAD) ** (-0.5)

    def one_type(t, carry):
        rows = pl.ds(pl.multiple_of(t * WIN, 16), WIN)
        field = x_ref[rows, :].astype(F32)
        hat1, scale1 = norm_parts(field)
        normed = (hat1 * g1_ref[...]).astype(BF)
        s_normed[rows, :] = normed
        triple[0:WIN, :] = dot(normed, wqkv_ref[...]).astype(BF)
        same = regq_ref[t] == regk_ref[t]
        for h in range(HEADS):
            q = triple[0:WIN, h * HEAD:(h + 1) * HEAD]
            k = triple[:, C + h * HEAD:C + (h + 1) * HEAD]
            v = triple[:, 2 * C + h * HEAD:2 * C + (h + 1) * HEAD]
            where_rows = pl.ds(t * HEADS + h, WIN, stride=TH)
            bias = jnp.concatenate(
                [bias_ref[0, where_rows, :], bias_ref[1, where_rows, :]], axis=1
            )
            scores = jnp.where(same, dot(q, k, NT) * root + bias, -1e30)
            weights = jnp.exp(scores - jnp.max(scores, axis=-1, keepdims=True))
            p = weights / jnp.sum(weights, axis=-1, keepdims=True)
            prob[h] = p
            mixed[:, h * HEAD:(h + 1) * HEAD] = dot(p.astype(BF), v).astype(BF)
        mixed_heads = mixed[...]
        s_mixed[rows, :] = mixed_heads
        branch = dot(mixed_heads, wproj_ref[...]).astype(BF).astype(F32)
        after = (field + branch).astype(BF).astype(F32)
        hat2, scale2 = norm_parts(after)
        nmlp = (hat2 * g2_ref[...]).astype(BF)
        s_nmlp[rows, :] = nmlp
        up = dot(nmlp, wup_ref[...])
        cdf = 0.5 * (1.0 + lax.erf(up * np.float32(np.sqrt(0.5))))
        slope = cdf + up * (jnp.exp(-0.5 * up * up) * np.float32(1 / np.sqrt(2 * np.pi)))
        hidden = (up * cdf).astype(BF)
        s_hidden[rows, :] = hidden
        after_mlp = (after + dot(hidden, wdown_ref[...])).astype(BF)

        spread = dot(perm_ref[...], after_mlp)
        parts = [spread[g * GPAD:(g + 1) * GPAD] for g in range(4)]
        average = sum(jnp.sum(p, axis=-1, keepdims=True) for p in parts) / (4 * C)
        parts = [p - average for p in parts]
        variance = sum(jnp.sum(p * p, axis=-1, keepdims=True) for p in parts) / (4 * C)
        scale = lax.rsqrt(variance + 1e-05)
        hats = [p * scale for p in parts]
        ct = ct_ref[t]
        merged = jnp.zeros((GPAD, 2 * C), F32)
        grads = []
        for g in range(4):
            gain = gm_ref[g:g + 1, :]
            weight = wm_ref[g * C:(g + 1) * C, :]
            nm = (hats[g] * gain).astype(BF)
            merged = merged + dot(nm, weight)
            s_merge[g * C:(g + 1) * C, :] += dot(nm, ct, TN)
            grads.append(dot(ct, weight, NT).astype(BF).astype(F32) * gain)
        merged_ref[t] = merged.astype(BF)
        first = sum(jnp.sum(g, axis=-1, keepdims=True) for g in grads) / (4 * C)
        second = sum(
            jnp.sum(g * hat, axis=-1, keepdims=True) for g, hat in zip(grads, hats)
        ) / (4 * C)
        back = jnp.concatenate(
            [scale * (g - first - hat * second) for g, hat in zip(grads, hats)], axis=0
        ).astype(BF)
        dy = dot(perm_ref[...], back, TN).astype(BF)

        s_dy[rows, :] = dy
        dhidden = dot(dy, wdown_ref[...], NT).astype(BF).astype(F32)
        du = (dhidden * slope).astype(BF)
        s_du[rows, :] = du
        dn = dot(du, wup_ref[...], NT).astype(BF).astype(F32) * g2_ref[...]
        da = (dy.astype(F32) + norm_grad(hat2, scale2, dn)).astype(BF)
        s_da[rows, :] = da

        dmixed[...] = dot(da, wproj_ref[...], NT).astype(BF)
        for h in range(HEADS):
            q = triple[0:WIN, h * HEAD:(h + 1) * HEAD]
            k = triple[:, C + h * HEAD:C + (h + 1) * HEAD]
            v = triple[:, 2 * C + h * HEAD:2 * C + (h + 1) * HEAD]
            dm = dmixed[:, h * HEAD:(h + 1) * HEAD]
            p = prob[h]
            dp = dot(dm, v, NT).astype(BF).astype(F32)
            ds = p * (dp - jnp.sum(dp * p, axis=-1, keepdims=True))
            where_rows = pl.ds(t * HEADS + h, WIN, stride=TH)
            dscore[0, where_rows, :] = ds[:, :LANES]
            dscore[1, where_rows, :] = ds[:, LANES:]
            dsb = (ds * root).astype(BF)
            dtriple[:, h * HEAD:(h + 1) * HEAD] = dot(dsb, k).astype(BF)
            dtriple[:, C + h * HEAD:C + (h + 1) * HEAD] = dot(dsb, q, TN)[:WIN].astype(BF)
            dtriple[:, 2 * C + h * HEAD:2 * C + (h + 1) * HEAD] = dot(
                p.astype(BF), dm, TN
            )[:WIN].astype(BF)
        dt = dtriple[...]
        s_dtriple[rows, :] = dt
        dn1 = dot(dt, wqkv_ref[...], NT).astype(BF).astype(F32) * g1_ref[...]
        fgrad_ref[rows, :] = (da.astype(F32) + norm_grad(hat1, scale1, dn1)).astype(BF)
        return carry

    lax.fori_loop(0, TYPES, one_type, 0)

    def pack(first_block, value):
        for b in range(value.shape[1] // LANES):
            start = (first_block + b) * C
            packed_ref[start:start + C, :] = value[:, b * LANES:(b + 1) * LANES].astype(BF)

    pack(0, jnp.concatenate(
        [dot(s_normed[...], s_dtriple[...], TN), dot(s_mixed[...], s_da[...], TN)], axis=1))
    pack(6, dot(s_nmlp[...], s_du[...], TN))
    down = dot(s_hidden[...], s_dy[...], TN)
    pack(12, jnp.concatenate([down[g * C:(g + 1) * C] for g in range(4)], axis=1))
    for g in range(4):
        pack(18 + 3 * g, s_merge[g * C:(g + 1) * C, :])

    s_table[...] = jnp.zeros_like(s_table)

    def row(i, carry):
        lane = lane_ref[pl.ds(i, 1), :]
        digit = digit_ref[pl.ds(i, 1), :]
        hot = (lax.broadcasted_iota(jnp.int32, (RADIX, KEYS), 0) == lane).astype(BF)
        rows = pl.ds(pl.multiple_of(i * TH, TH), TH)
        ds = jnp.concatenate([dscore[0, rows, :], dscore[1, rows, :]], axis=1)
        left = jnp.concatenate(
            [jnp.where(digit == d, ds, 0.0) for d in range(DIGITS)], axis=0
        ).astype(BF)
        s_table[...] += dot(left, hot, NT)
        return carry

    lax.fori_loop(0, WIN, row, 0)
    for b in range(2):
        start = ROWS_W + b * DIGITS * TH
        packed_ref[start:start + DIGITS * TH, :] = s_table[:, b * LANES:(b + 1) * LANES].astype(BF)
    end = ROWS_W + ROWS_T
    if packed_ref.shape[0] > end:
        packed_ref[end:, :] = jnp.zeros((packed_ref.shape[0] - end, LANES), BF)


def reduce_kernel(
    n, share, factor, packed_ref,
    qkv_ref, proj_ref, up_ref, down_ref, merge_ref, table_ref,
    arrived, gathered, send1, recv1, send2, recv2,
):
    me = lax.axis_index("lon")
    barrier = pltpu.get_barrier_semaphore()
    for k in range(1, n):
        pl.semaphore_signal(
            barrier, inc=1, device_id={"lon": lax.rem(me + k, n)},
            device_id_type=pl.DeviceIdType.MESH,
        )
    pl.semaphore_wait(barrier, n - 1)

    def rows_of(device):
        return pl.ds(pl.multiple_of(device * share, 16), share)

    first = []
    for k in range(1, n):
        peer = lax.rem(me + k, n)
        copy = pltpu.make_async_remote_copy(
            src_ref=packed_ref.at[rows_of(peer), :], dst_ref=arrived.at[k],
            send_sem=send1.at[k], recv_sem=recv1.at[k],
            device_id={"lon": peer}, device_id_type=pl.DeviceIdType.MESH,
        )
        copy.start()
        first.append(copy)
    for copy in first:
        copy.wait_recv()
    total = packed_ref[rows_of(me), :].astype(F32)
    for k in range(1, n):
        total = total + arrived[k].astype(F32)
    gathered[rows_of(me), :] = total.astype(BF)
    second = []
    for k in range(1, n):
        copy = pltpu.make_async_remote_copy(
            src_ref=gathered.at[rows_of(me), :], dst_ref=gathered.at[rows_of(me), :],
            send_sem=send2.at[k], recv_sem=recv2.at[k],
            device_id={"lon": lax.rem(me + k, n)}, device_id_type=pl.DeviceIdType.MESH,
        )
        copy.start()
        second.append(copy)
    for copy in first:
        copy.wait_send()
    for copy in second:
        copy.wait()

    def block(index):
        return gathered[index * C:(index + 1) * C, :].astype(F32) * factor

    def joined(start, count):
        return jnp.concatenate([block(start + b) for b in range(count)], axis=1)

    front = joined(0, 6)
    qkv_ref[...] = front[:, :3 * C]
    proj_ref[...] = front[:, 3 * C:]
    up_ref[...] = joined(6, 6)
    downs = joined(12, 6)
    for g in range(4):
        down_ref[g * C:(g + 1) * C, :] = downs[:, g * C:(g + 1) * C]
        merge_ref[g * C:(g + 1) * C, :] = joined(18 + 3 * g, 3)
    for b in range(2):
        start = ROWS_W + b * DIGITS * TH
        half = gathered[start:start + DIGITS * TH, :].astype(F32) * factor
        for d in range(DIGITS):
            at = d * RADIX + b * LANES
            table_ref[:, at:at + LANES] = half[d * TH:(d + 1) * TH]


def passed_along(value, axis, steps):
    count = lax.axis_size(axis)
    return lax.ppermute(value, axis, [(s, (s + steps) % count) for s in range(count)])


def group_order():
    order = np.zeros((4 * GPAD, WIN), np.float32)
    for pa in range(2):
        for pb in range(2):
            for z in range(WZ):
                for a in range(WLAT // 2):
                    for b in range(WLON // 2):
                        cell = (z * (WLAT // 2) + a) * (WLON // 2) + b
                        token = (z * WLAT + 2 * a + pa) * WLON + 2 * b + pb
                        order[(2 * pa + pb) * GPAD + cell, token] = 1.0
    return jnp.asarray(order, BF)


def local(
    fields, norm_gain, qkv_weight, proj_weight, bias_table, bias_index, region_ids,
    mlp_gain, up_weight, down_weight, merge_gain, merge_weight, cotangent,
):
    n = lax.axis_size("lon")
    windows = fields.shape[2] // WLON
    assert windows == 1
    bands = LAT // WLAT
    west_fields = passed_along(fields[:, :, :HALF], "lon", -1)
    west_ct = passed_along(cotangent[:, :, :HALF // 2], "lon", -1)

    table = jnp.pad(bias_table.reshape(TH, BPOS), ((0, 0), (0, DIGITS * RADIX - BPOS)))
    table = table.reshape(TH, DIGITS, RADIX).transpose(1, 0, 2).reshape(DIGITS * TH, RADIX)
    high = lax.reduce_precision(table, 8, 7)
    low = (table - high).astype(BF)
    high = high.astype(BF)
    index = jnp.pad(bias_index, ((0, 0), (0, KEYS - WIN)), constant_values=-1)
    digit = index >> 8
    lane = jnp.where(index < 0, -1, index & (RADIX - 1))
    bias = pl.pallas_call(
        bias_kernel,
        out_shape=jax.ShapeDtypeStruct((2, WIN * TH, LANES), F32),
        in_specs=[VMEM] * 4,
        out_specs=VMEM,
        compiler_params=pltpu.CompilerParams(vmem_limit_bytes=24 << 20),
        cost_estimate=pl.CostEstimate(flops=14_000_000_000, bytes_accessed=4 << 20, transcendentals=0),
        name="bias_rows",
    )(high, low, digit, lane)

    labels = region_ids.reshape(WZ, bands, WLAT).transpose(1, 0, 2).reshape(TYPES, WZ * WLAT)
    labels = jnp.repeat(labels, WLON, axis=1)
    label_keys = jnp.pad(labels, ((0, 0), (0, KEYS - WIN)), constant_values=-1)

    shifted = jnp.concatenate([fields[:, :, HALF:], west_fields], axis=2)
    tokens = shifted.reshape(WZ, bands, WLAT, WLON, C).transpose(1, 0, 2, 3, 4).reshape(TYPES * WIN, C)
    ct = jnp.concatenate([cotangent[:, :, HALF // 2:], west_ct], axis=2)
    ct = ct.reshape(WZ, bands, WLAT // 2, WLON // 2, 2 * C).transpose(1, 0, 2, 3, 4)
    ct = jnp.pad(ct.reshape(TYPES, GROUP, 2 * C), ((0, 0), (0, GPAD - GROUP), (0, 0)))

    share = -(-(ROWS_W + ROWS_T) // (16 * n)) * 16
    total_rows = TYPES * WIN
    merged_win, fgrad_win, packed = pl.pallas_call(
        block_kernel,
        out_shape=(
            jax.ShapeDtypeStruct((TYPES, GPAD, 2 * C), BF),
            jax.ShapeDtypeStruct((total_rows, C), BF),
            jax.ShapeDtypeStruct((n * share, LANES), BF),
        ),
        in_specs=[VMEM] * 16,
        out_specs=(VMEM,) * 3,
        scratch_shapes=[
            pltpu.VMEM((KEYS, 3 * C), BF),
            pltpu.VMEM((HEADS, WIN, KEYS), F32),
            pltpu.VMEM((WIN, C), BF),
            pltpu.VMEM((WIN, C), BF),
            pltpu.VMEM((WIN, 3 * C), BF),
            pltpu.VMEM((2, WIN * TH, LANES), F32),
            pltpu.VMEM((total_rows, C), BF),
            pltpu.VMEM((total_rows, 3 * C), BF),
            pltpu.VMEM((total_rows, C), BF),
            pltpu.VMEM((total_rows, C), BF),
            pltpu.VMEM((total_rows, C), BF),
            pltpu.VMEM((total_rows, MLP), BF),
            pltpu.VMEM((total_rows, MLP), BF),
            pltpu.VMEM((total_rows, C), BF),
            pltpu.VMEM((4 * C, 2 * C), F32),
            pltpu.VMEM((DIGITS * TH, RADIX), F32),
        ],
        compiler_params=pltpu.CompilerParams(vmem_limit_bytes=48 << 20),
        cost_estimate=pl.CostEstimate(flops=20_000_000_000, bytes_accessed=8 << 20, transcendentals=2_000_000),
        name="block",
    )(
        tokens, ct, bias, labels[:, :, None], label_keys[:, None, :], digit, lane, group_order(),
        norm_gain[None], qkv_weight, proj_weight, mlp_gain[None], up_weight, down_weight,
        merge_gain.reshape(4, C), merge_weight,
    )

    merged_grid = merged_win[:, :GROUP].reshape(bands, WZ, WLAT // 2, WLON // 2, 2 * C)
    merged_grid = merged_grid.transpose(1, 0, 2, 3, 4).reshape(Z, LAT // 2, WLON // 2, 2 * C)
    fgrad_grid = fgrad_win.reshape(bands, WZ, WLAT, WLON, C)
    fgrad_grid = fgrad_grid.transpose(1, 0, 2, 3, 4).reshape(Z, LAT, WLON, C)
    east_merged = passed_along(merged_grid[:, :, HALF // 2:], "lon", 1)
    east_fgrad = passed_along(fgrad_grid[:, :, HALF:], "lon", 1)
    merged = jnp.concatenate([east_merged, merged_grid[:, :, :HALF // 2]], axis=2)
    field_grad = jnp.concatenate([east_fgrad, fgrad_grid[:, :, :HALF]], axis=2)

    factor = float(Z * LAT * fields.shape[2] * n) ** (-0.5)
    outs = pl.pallas_call(
        functools.partial(reduce_kernel, n, share, factor),
        out_shape=(
            jax.ShapeDtypeStruct((C, 3 * C), F32),
            jax.ShapeDtypeStruct((C, C), F32),
            jax.ShapeDtypeStruct((C, MLP), F32),
            jax.ShapeDtypeStruct((MLP, C), F32),
            jax.ShapeDtypeStruct((4 * C, 2 * C), F32),
            jax.ShapeDtypeStruct((TH, DIGITS * RADIX), F32),
        ),
        in_specs=[VMEM],
        out_specs=(VMEM,) * 6,
        scratch_shapes=[
            pltpu.VMEM((n, share, LANES), BF),
            pltpu.VMEM((n * share, LANES), BF),
            pltpu.SemaphoreType.DMA((n,)),
            pltpu.SemaphoreType.DMA((n,)),
            pltpu.SemaphoreType.DMA((n,)),
            pltpu.SemaphoreType.DMA((n,)),
        ],
        compiler_params=pltpu.CompilerParams(
            collective_id=0, has_side_effects=True, vmem_limit_bytes=24 << 20
        ),
        cost_estimate=pl.CostEstimate(flops=10_000_000_000, bytes_accessed=16 << 20, transcendentals=0),
        name="weight_sums",
    )(packed)
    qkv_grad, proj_grad, up_grad, down_grad, merge_grad, table_grad = outs
    table_grad = table_grad[:, :BPOS].reshape(TYPES, HEADS, BPOS)
    return (
        merged, field_grad, qkv_grad, proj_grad, up_grad, down_grad, merge_grad, table_grad,
    )


def solution(mesh):
    grid = P("groups", None, "lon", None)
    rows = P("groups", None)
    return jax.shard_map(
        local,
        mesh=mesh,
        in_specs=(grid,) + (P(),) * 11 + (grid,),
        out_specs=(grid, grid) + (rows,) * 5 + (P("groups", None, None),),
        check_vma=False,
    )
```

profile of v0, /device:TPU:27, one launch (start us, length us, event | category | flops | bytes accessed | tf_op | source)
XLA Modules:
  0.0 210.2 jit_solution(3409308619119212901)
XLA Ops:
  0.6 0.9 fusion.4
  1.6 0.7 collective-permute-start.1
  2.3 1.0 fusion.2
  3.3 0.1 collective-permute-start
  3.4 0.9 and_select_fusion
  4.3 1.1 copy.48
  5.5 0.1 reshape.69
  5.6 0.2 copy.49
  5.8 35.8 %bias_rows.1.bias_ref = f32[2,3456,128]{2,1,0:T(8,128)S(1)} custom-call(bf16[312,256]{1,0:T(8,128)(2,1)S(1)} %get-tuple-element.51.high_ref, bf16[312,256]{1,0:T(8,128)(2,1)S(1)} %get-tuple-element.50.low_ref, s32[144,256]{1,0:T(8,128)S(1)} %get-tuple-element.57.digit_ref, s32[144,256]{1,0:T(8,128)S(1)} %get-tuple-element.56.lane_ref), custom_call_target="tpu_custom_call" | custom-call | flops 14000000000 | bytes 4194304 | tf_op jit(solution)/shard_map/bias_rows/pallas_call | solution.py:328
  41.6 1.7 copy-done.9
  43.4 0.1 reshape.71
  43.5 0.1 reshape.72
  43.5 0.1 broadcast_in_dim.17
  43.6 0.1 reshape.73
  43.7 0.1 broadcast_in_dim_reshape.4.regq_ref
  43.9 0.1 reshape.74.gm_ref
  44.0 0.2 copy.52.wdown_ref
  44.1 0.1 pad_maximum_fusion.2
  44.4 0.0 copy-start.8
  44.5 0.1 pad_maximum_fusion
  44.6 0.3 copy.44
  44.9 0.1 reshape.65.x_ref
  45.1 0.3 copy-done.2
  45.4 0.1 copy-done.3
  45.4 0.1 copy-done.4
  45.5 0.0 copy-done.5
  45.5 0.1 copy-done.8
  45.6 66.3 %block.1 = (bf16[4,48,384]{2,1,0:T(8,128)(2,1)S(1)}, bf16[576,192]{1,0:T(8,128)(2,1)S(1)}, bf16[6400,128]{1,0:T(8,128)(2,1)S(1)}) custom-call(bf16[576,192]{1,0:T(8,128)(2,1)S(1)} %reshape.65.x_ref, bf16[4,48,384]{2,1,0:T(8,128)(2,1)S(1)} %pad.16.ct_ref, f32[2,3456,128]{2,1,0:T(8,128)} %copy-done.9, s32[4,144,1]{2,1,0:T(8,128)S(1)} %broadcast_in_dim_reshape.4.regq_ref, ...), custom_call_target="tpu_custom_call" | custom-call | flops 20000000000 | bytes 8388608 | tf_op jit(solution)/shard_map/block/pallas_call | solution.py:350
  111.9 1.2 copy-done.10
  113.2 0.1 copy.54
  113.3 0.7 fusion.3
  114.0 4.4 %collective-permute-start.2 = (bf16[2,12,3,384]{3,0,2,1:T(2,128)(2,1)}, bf16[2,12,3,384]{3,0,2,1:T(2,128)(2,1)}, u32[]{:S(2)}, u32[]{:S(2)}) collective-permute-start(bf16[2,12,3,384]{3,0,2,1:T(2,128)(2,1)} %get-tuple-element.58), channel_id=1, source_target_pairs={{0,1},{1,2},{2,3},{3,4},{4,5},{5,6},{6,7},{7,8},{8,9},{9,10},{10,1... | collective-permute-start | bytes 165896 | tf_op jit(solution)/shard_map/ppermute | solution.py:293
  118.4 0.1 reshape.77
  118.5 0.3 copy.55
  118.8 0.9 fusion.1
  119.7 1.4 copy-done.11
  121.1 77.6 %weight_sums.1 = (f32[192,576]{1,0:T(8,128)S(1)}, f32[192,192]{1,0:T(8,128)S(1)}, f32[192,768]{1,0:T(8,128)S(1)}, f32[768,192]{1,0:T(8,128)S(1)}, f32[768,384]{1,0:T(8,128)S(1)}, /*index=5*/f32[24,3328]{1,0:T(8,128)S(1)}) custom-call(bf16[6400,128]{1,0:T(8,128)(2,1)S(1)} %copy-done.11), custom_call_target="tpu_custom_call" | custom-call | flops 10000000000 | bytes 16777216 | tf_op jit(solution)/shard_map/weight_sums/pallas_call | solution.py:396
  198.8 0.7 copy-done
  199.4 0.8 reshape.79
  200.2 1.9 copy.58
  202.1 1.1 copy.57
  203.2 1.6 pad_maximum_fusion.3
  204.8 1.3 pad_maximum_fusion.1
  206.1 0.8 copy.56
  206.9 0.8 copy.63
  207.6 0.7 copy.64
  208.3 0.8 copy.65
  209.1 1.0 copy.66
  (39 shorter events, 0.4 us)
Async XLA Ops:
  1.6 42.6 %collective-permute-start.1 = (bf16[2,12,3,384]{3,0,2,1:T(2,128)(2,1)S(1)}, bf16[2,12,3,384]{3,0,2,1:T(2,128)(2,1)S(1)}, u32[]{:S(2)}, u32[]{:S(2)}) collective-permute-start(bf16[2,12,3,384]{3,0,2,1:T(2,128)(2,1)S(1)} %get-tuple-element.61), channel_id=1, source_target_pairs={{0,15},{1,0},{2,1},{3,2},{4,3},{5,4},{6,5},{7,6},{8,7},{9,8},{10,9... | collective-permute-start | bytes 165896 | tf_op jit(solution)/shard_map/ppermute | solution.py:293
  3.3 41.2 %collective-permute-start = (bf16[2,24,6,192]{3,1,2,0:T(8,128)(2,1)S(1)}, bf16[2,24,6,192]{3,1,2,0:T(8,128)(2,1)S(1)}, u32[]{:S(2)}, u32[]{:S(2)}) collective-permute-start(bf16[2,24,6,192]{3,1,2,0:T(8,128)(2,1)S(1)} %get-tuple-element.55), channel_id=1, source_target_pairs={{0,15},{1,0},{2,1},{3,2},{4,3},{5,4},{6,5},{7,6},{8,7},{9,8},{10,9... | collective-permute-start | bytes 331784 | tf_op jit(solution)/shard_map/ppermute | solution.py:293
  5.8 37.6 %copy-start.15 = (s32[2,24]{1,0:T(2,128)S(1)}, s32[2,24]{1,0:T(2,128)}, u32[]{:S(2)}) copy-start(s32[2,24]{1,0:T(2,128)} %param.20) | copy-start | bytes 580
  5.8 38.0 %copy-start.14 = (f32[768]{0:T(1024)S(1)}, f32[768]{0:T(1024)}, u32[]{:S(2)}) copy-start(f32[768]{0:T(1024)} %param.24) | copy-start | bytes 9220
  5.8 38.1 %copy-start.12 = (bf16[768,192]{0,1:T(8,128)(2,1)S(1)}, bf16[768,192]{0,1:T(8,128)(2,1)}, u32[]{:S(2)}) copy-start(bf16[768,192]{0,1:T(8,128)(2,1)} %param.23) | copy-start | bytes 884740
  41.6 1.7 copy-start.9
  44.3 1.1 copy-start.2
  44.3 1.1 copy-start.3
  44.3 1.2 copy-start.4
  44.3 1.2 copy-start.5
  44.4 1.2 copy-start.6
  44.4 1.2 copy-start.7
  44.4 1.2 copy-start.8
  111.9 1.2 copy-start.10
  114.0 89.1 %collective-permute-start.2 = (bf16[2,12,3,384]{3,0,2,1:T(2,128)(2,1)}, bf16[2,12,3,384]{3,0,2,1:T(2,128)(2,1)}, u32[]{:S(2)}, u32[]{:S(2)}) collective-permute-start(bf16[2,12,3,384]{3,0,2,1:T(2,128)(2,1)} %get-tuple-element.58), channel_id=1, source_target_pairs={{0,1},{1,2},{2,3},{3,4},{4,5},{5,6},{6,7},{7,8},{8,9},{9,10},{10,1... | collective-permute-start | bytes 165896 | tf_op jit(solution)/shard_map/ppermute | solution.py:293
  119.7 85.1 %collective-permute-start.3 = (bf16[2,24,6,192]{3,0,2,1:T(2,128)(2,1)}, bf16[2,24,6,192]{3,0,2,1:T(2,128)(2,1)}, u32[]{:S(2)}, u32[]{:S(2)}) collective-permute-start(bf16[2,24,6,192]{3,0,2,1:T(2,128)(2,1)} %get-tuple-element.52), channel_id=1, source_target_pairs={{0,1},{1,2},{2,3},{3,4},{4,5},{5,6},{6,7},{7,8},{8,9},{9,10},{10,1... | collective-permute-start | bytes 331784 | tf_op jit(solution)/shard_map/ppermute | solution.py:293
  119.7 1.4 copy-start.11
  198.7 0.7 copy-start
  200.2 2.9 %copy-start.13 = (bf16[2,12,3,384]{3,0,2,1:T(2,128)(2,1)S(1)}, bf16[2,12,3,384]{3,0,2,1:T(2,128)(2,1)}, u32[]{:S(2)}) copy-start(bf16[2,12,3,384]{3,0,2,1:T(2,128)(2,1)} %get-tuple-element.59) | copy-start | bytes 165892
  202.1 5.6 %copy-start.1 = (f32[192,192]{1,0:T(8,128)S(1)}, f32[192,192]{1,0:T(8,128)}, u32[]{:S(2)}) copy-start(f32[192,192]{1,0:T(8,128)} %copy-done) | copy-start | bytes 442372
where the time goes:
time: 211 us; the launch traced here: 210 us
  Pallas kernels  180 us (85%)
  local copies, waits for them, and re-layouts  20.2 us (10%)
  starting transfers between devices  5.23 us (2%)
  other arithmetic  4.12 us (2%)
    pallas_call x1, Pallas kernels, local(): pl.pallas_call(functools.partial(reduce_kernel, n, share, factor), out_sh...  77.6 us
    pallas_call x1, Pallas kernels, local(): pl.pallas_call(block_kernel, out_shape=(jax.ShapeDtypeStruct((TYPES, GPAD...  66.3 us
    pallas_call x1, Pallas kernels, local(): pl.pallas_call(bias_kernel, out_shape=jax.ShapeDtypeStruct((2, WIN * TH,...  35.8 us
    unnamed x41, local copies, waits for them, and re-layouts  13.8 us
    ppermute x4, starting transfers between devices, passed_along(): lax.ppermute(value, axis, [(s, (s + steps) % count) for s in range(count)])  5.23 us
  transfers between devices with their start and end apart: 4, of which 0 were waited for; matrix products, arithmetic and copies ran while one was open for 5% of the time, Pallas kernels for 54%

commit v1 on v0

--- a/solution.py
+++ b/solution.py
@@ -30,6 +30,7 @@
 GPAD = 48
 ROWS_W = 30 * C
 ROWS_T = DIGITS * TH * 2
+UNROLL = 4
 BF = jnp.bfloat16
 F32 = jnp.float32
 VMEM = pl.BlockSpec(memory_space=pltpu.VMEM)
@@ -43,23 +44,23 @@
 TN = ((0,), (0,))
 
 
-def bias_kernel(high_ref, low_ref, digit_ref, lane_ref, out_ref):
-    def row(i, carry):
-        lane = lane_ref[pl.ds(i, 1), :]
-        digit = digit_ref[pl.ds(i, 1), :]
-        hot = (lax.broadcasted_iota(jnp.int32, (RADIX, KEYS), 0) == lane).astype(BF)
-        high = dot(high_ref[...], hot)
-        low = dot(low_ref[...], hot)
-        total = jnp.zeros((TH, KEYS), F32)
-        for d in range(DIGITS):
-            piece = high[d * TH:(d + 1) * TH] + low[d * TH:(d + 1) * TH]
-            total = jnp.where(digit == d, piece, total)
-        rows = pl.ds(pl.multiple_of(i * TH, TH), TH)
-        out_ref[0, rows, :] = total[:, :LANES]
-        out_ref[1, rows, :] = total[:, LANES:]
+def bias_kernel(table_ref, digit_ref, lane_ref, out_ref):
+    def some_rows(step, carry):
+        for u in range(UNROLL):
+            i = step * UNROLL + u
+            lane = lane_ref[pl.ds(i, 1), :]
+            digit = digit_ref[pl.ds(i, 1), :]
+            hot = (lax.broadcasted_iota(jnp.int32, (RADIX, KEYS), 0) == lane).astype(BF)
+            found = dot(table_ref[...], hot)
+            total = jnp.zeros((TH, KEYS), F32)
+            for d in range(DIGITS):
+                total = jnp.where(digit == d, found[d * TH:(d + 1) * TH], total)
+            rows = pl.ds(pl.multiple_of(i * TH, TH), TH)
+            out_ref[0, rows, :] = total[:, :LANES]
+            out_ref[1, rows, :] = total[:, LANES:]
         return carry
 
-    lax.fori_loop(0, WIN, row, 0)
+    lax.fori_loop(0, WIN // UNROLL, some_rows, 0)
 
 
 def norm_parts(values):
@@ -198,19 +199,24 @@
 
     s_table[...] = jnp.zeros_like(s_table)
 
-    def row(i, carry):
-        lane = lane_ref[pl.ds(i, 1), :]
-        digit = digit_ref[pl.ds(i, 1), :]
-        hot = (lax.broadcasted_iota(jnp.int32, (RADIX, KEYS), 0) == lane).astype(BF)
-        rows = pl.ds(pl.multiple_of(i * TH, TH), TH)
-        ds = jnp.concatenate([dscore[0, rows, :], dscore[1, rows, :]], axis=1)
-        left = jnp.concatenate(
-            [jnp.where(digit == d, ds, 0.0) for d in range(DIGITS)], axis=0
-        ).astype(BF)
-        s_table[...] += dot(left, hot, NT)
+    def some_rows(step, carry):
+        hots, lefts = [], []
+        for u in range(UNROLL):
+            i = step * UNROLL + u
+            lane = lane_ref[pl.ds(i, 1), :]
+            digit = digit_ref[pl.ds(i, 1), :]
+            hots.append((lax.broadcasted_iota(jnp.int32, (RADIX, KEYS), 0) == lane).astype(BF))
+            rows = pl.ds(pl.multiple_of(i * TH, TH), TH)
+            ds = jnp.concatenate([dscore[0, rows, :], dscore[1, rows, :]], axis=1)
+            lefts.append(jnp.concatenate(
+                [jnp.where(digit == d, ds, 0.0) for d in range(DIGITS)], axis=0
+            ).astype(BF))
+        s_table[...] += dot(
+            jnp.concatenate(lefts, axis=1), jnp.concatenate(hots, axis=1), NT
+        )
         return carry
 
-    lax.fori_loop(0, WIN, row, 0)
+    lax.fori_loop(0, WIN // UNROLL, some_rows, 0)
     for b in range(2):
         start = ROWS_W + b * DIGITS * TH
         packed_ref[start:start + DIGITS * TH, :] = s_table[:, b * LANES:(b + 1) * LANES].astype(BF)
@@ -222,48 +228,80 @@
 def reduce_kernel(
     n, share, factor, packed_ref,
     qkv_ref, proj_ref, up_ref, down_ref, merge_ref, table_ref,
-    arrived, gathered, send1, recv1, send2, recv2,
+    paired, pair_sum, arrived, gathered,
+    send0, recv0, send1, recv1, send2, recv2, send3, recv3,
 ):
+    chips = n // 2
     me = lax.axis_index("lon")
-    barrier = pltpu.get_barrier_semaphore()
-    for k in range(1, n):
-        pl.semaphore_signal(
-            barrier, inc=1, device_id={"lon": lax.rem(me + k, n)},
-            device_id_type=pl.DeviceIdType.MESH,
-        )
-    pl.semaphore_wait(barrier, n - 1)
-
-    def rows_of(device):
-        return pl.ds(pl.multiple_of(device * share, 16), share)
-
-    first = []
-    for k in range(1, n):
-        peer = lax.rem(me + k, n)
+    chip, core = me // 2, lax.rem(me, 2)
+    partner = 2 * chip + 1 - core
+
+    def across(k):
+        return 2 * lax.rem(chip + k, chips) + core
+
+    def rows_of(half, index):
+        return pl.ds(pl.multiple_of((half * chips + index) * share, 16), share)
+
+    def sent(src, dst, send, recv, device):
         copy = pltpu.make_async_remote_copy(
-            src_ref=packed_ref.at[rows_of(peer), :], dst_ref=arrived.at[k],
-            send_sem=send1.at[k], recv_sem=recv1.at[k],
-            device_id={"lon": peer}, device_id_type=pl.DeviceIdType.MESH,
+            src_ref=src, dst_ref=dst, send_sem=send, recv_sem=recv,
+            device_id={"lon": device}, device_id_type=pl.DeviceIdType.MESH,
         )
         copy.start()
-        first.append(copy)
-    for copy in first:
-        copy.wait_recv()
-    total = packed_ref[rows_of(me), :].astype(F32)
-    for k in range(1, n):
+        return copy
+
+    barrier = pltpu.get_barrier_semaphore()
+    for device in [partner] + [across(k) for k in range(1, chips)]:
+        pl.semaphore_signal(
+            barrier, inc=1, device_id={"lon": device}, device_id_type=pl.DeviceIdType.MESH
+        )
+    pl.semaphore_wait(barrier, chips)
+
+    order = list(range(1, chips)) + [0]
+    stage0 = {}
+    for k in order:
+        stage0[k] = sent(
+            packed_ref.at[rows_of(1 - core, lax.rem(chip + k, chips)), :],
+            paired.at[k], send0.at[k], recv0.at[k], partner,
+        )
+    stage1 = {}
+    total = None
+    for k in order:
+        stage0[k].wait_recv()
+        own = packed_ref[rows_of(core, lax.rem(chip + k, chips)), :].astype(F32)
+        summed = own + paired[k].astype(F32)
+        if k == 0:
+            total = summed
+        else:
+            pair_sum[k] = summed.astype(BF)
+            stage1[k] = sent(
+                pair_sum.at[k], arrived.at[k], send1.at[k], recv1.at[k], across(k)
+            )
+    for k in range(1, chips):
+        stage1[k].wait_recv()
         total = total + arrived[k].astype(F32)
-    gathered[rows_of(me), :] = total.astype(BF)
-    second = []
-    for k in range(1, n):
-        copy = pltpu.make_async_remote_copy(
-            src_ref=gathered.at[rows_of(me), :], dst_ref=gathered.at[rows_of(me), :],
-            send_sem=send2.at[k], recv_sem=recv2.at[k],
-            device_id={"lon": lax.rem(me + k, n)}, device_id_type=pl.DeviceIdType.MESH,
+    mine = rows_of(core, chip)
+    gathered[mine, :] = total.astype(BF)
+    stage2 = {}
+    for k in range(1, chips):
+        stage2[k] = sent(
+            gathered.at[mine, :], gathered.at[mine, :], send2.at[k], recv2.at[k], across(k)
         )
-        copy.start()
-        second.append(copy)
-    for copy in first:
-        copy.wait_send()
-    for copy in second:
+    stage3 = [sent(
+        gathered.at[mine, :], gathered.at[mine, :], send3.at[0], recv3.at[0], partner
+    )]
+    for k in range(1, chips):
+        stage2[k].wait_recv()
+        rows = rows_of(core, lax.rem(chip - k + chips, chips))
+        stage3.append(sent(
+            gathered.at[rows, :], gathered.at[rows, :], send3.at[k], recv3.at[k], partner
+        ))
+    for k in order:
+        stage0[k].wait_send()
+    for k in range(1, chips):
+        stage1[k].wait_send()
+        stage2[k].wait_send()
+    for copy in stage3:
         copy.wait()
 
     def block(index):
@@ -319,21 +357,19 @@
 
     table = jnp.pad(bias_table.reshape(TH, BPOS), ((0, 0), (0, DIGITS * RADIX - BPOS)))
     table = table.reshape(TH, DIGITS, RADIX).transpose(1, 0, 2).reshape(DIGITS * TH, RADIX)
-    high = lax.reduce_precision(table, 8, 7)
-    low = (table - high).astype(BF)
-    high = high.astype(BF)
+    table = table.astype(BF)
     index = jnp.pad(bias_index, ((0, 0), (0, KEYS - WIN)), constant_values=-1)
     digit = index >> 8
     lane = jnp.where(index < 0, -1, index & (RADIX - 1))
     bias = pl.pallas_call(
         bias_kernel,
         out_shape=jax.ShapeDtypeStruct((2, WIN * TH, LANES), F32),
-        in_specs=[VMEM] * 4,
+        in_specs=[VMEM] * 3,
         out_specs=VMEM,
         compiler_params=pltpu.CompilerParams(vmem_limit_bytes=24 << 20),
-        cost_estimate=pl.CostEstimate(flops=14_000_000_000, bytes_accessed=4 << 20, transcendentals=0),
+        cost_estimate=pl.CostEstimate(flops=7_000_000_000, bytes_accessed=4 << 20, transcendentals=0),
         name="bias_rows",
-    )(high, low, digit, lane)
+    )(table, digit, lane)
 
     labels = region_ids.reshape(WZ, bands, WLAT).transpose(1, 0, 2).reshape(TYPES, WZ * WLAT)
     labels = jnp.repeat(labels, WLON, axis=1)
@@ -406,13 +442,11 @@
         in_specs=[VMEM],
         out_specs=(VMEM,) * 6,
         scratch_shapes=[
-            pltpu.VMEM((n, share, LANES), BF),
+            pltpu.VMEM((n // 2, share, LANES), BF),
+            pltpu.VMEM((n // 2, share, LANES), BF),
+            pltpu.VMEM((n // 2, share, LANES), BF),
             pltpu.VMEM((n * share, LANES), BF),
-            pltpu.SemaphoreType.DMA((n,)),
-            pltpu.SemaphoreType.DMA((n,)),
-            pltpu.SemaphoreType.DMA((n,)),
-            pltpu.SemaphoreType.DMA((n,)),
-        ],
+        ] + [pltpu.SemaphoreType.DMA((n // 2,))] * 8,
         compiler_params=pltpu.CompilerParams(
             collective_id=0, has_side_effects=True, vmem_limit_bytes=24 << 20
         ),

time: 211 us -> 133 us (0.63)
  Pallas kernels: 180 us -> 103 us
    pallas_call x1, Pallas kernels: 77.6 us -> 46.4 us  [local(): pl.pallas_call(functools.partial(reduce_kernel, n, share, factor), out_sh...]
    pallas_call x1, Pallas kernels: 35.8 us -> 12.2 us  [local(): pl.pallas_call(bias_kernel, out_shape=jax.ShapeDtypeStruct((2, WIN * TH,...]
    pallas_call x1, Pallas kernels: 66.3 us -> 44.5 us  [local(): pl.pallas_call(block_kernel, out_shape=(jax.ShapeDtypeStruct((TYPES, GPAD...]
    unnamed x41 -> x42, local copies, waits for them, and re-layouts: 13.8 us -> 12.8 us
  transfers between devices with their start and end apart: 4 -> 4, of which waited for: 0 -> 0; matrix products, arithmetic and copies ran while one was open for 5% -> 7% of each run, Pallas kernels for 54% -> 44%
where the time goes in v1:
time: 133 us
  Pallas kernels  103 us (77%)
  local copies, waits for them, and re-layouts  19.1 us (14%)
  starting transfers between devices  5.23 us (4%)
  other arithmetic  4.2 us (3%)
    pallas_call x1, Pallas kernels, local(): pl.pallas_call(functools.partial(reduce_kernel, n, share, factor), out_sh...  46.4 us
    pallas_call x1, Pallas kernels, local(): pl.pallas_call(block_kernel, out_shape=(jax.ShapeDtypeStruct((TYPES, GPAD...  44.5 us
    unnamed x42, local copies, waits for them, and re-layouts  12.8 us
    pallas_call x1, Pallas kernels, local(): pl.pallas_call(bias_kernel, out_shape=jax.ShapeDtypeStruct((2, WIN * TH,...  12.2 us
    ppermute x4, starting transfers between devices, passed_along(): lax.ppermute(value, axis, [(s, (s + steps) % count) for s in range(count)])  5.23 us
  transfers between devices with their start and end apart: 4, of which 0 were waited for; matrix products, arithmetic and copies ran while one was open for 7% of the time, Pallas kernels for 44%

profile of v1, /device:TPU:27, one launch (start us, length us, event | category | flops | bytes accessed | tf_op | source)
XLA Modules:
  0.0 132.6 jit_solution(4272041722288261952)
XLA Ops:
  0.6 1.0 fusion.3
  1.6 0.7 collective-permute-start.1
  2.3 1.0 fusion.1
  3.3 0.1 collective-permute-start
  3.4 1.0 convert.5
  4.5 0.1 reshape.67
  4.6 0.1 convert_element_type.11
  4.7 0.1 copy.49
  4.9 12.2 %bias_rows.1.bias_ref = f32[2,3456,128]{2,1,0:T(8,128)S(1)} custom-call(bf16[312,256]{1,0:T(8,128)(2,1)S(1)} %bitcast.20, s32[144,256]{1,0:T(8,128)S(1)} %get-tuple-element.55.digit_ref, s32[144,256]{1,0:T(8,128)S(1)} %get-tuple-element.54.lane_ref), custom_call_target="tpu_custom_call" | custom-call | flops 7000000000 | bytes 4194304 | tf_op jit(solution)/shard_map/bias_rows/pallas_call | solution.py:364
  17.1 1.7 %copy-done.9 = f32[2,3456,128]{2,1,0:T(8,128)} copy-done((f32[2,3456,128]{2,1,0:T(8,128)}, f32[2,3456,128]{2,1,0:T(8,128)S(1)}, u32[]{:S(2)}) %copy-start.9) | copy-done | bytes 3538968
  18.8 0.1 reshape.68
  18.9 0.1 reshape.69
  19.0 0.1 broadcast_in_dim.17
  19.0 0.1 reshape.70
  19.1 0.1 broadcast_in_dim_reshape.4.regq_ref
  19.3 0.1 reshape.71.gm_ref
  19.4 0.2 copy.52.wdown_ref
  19.6 0.1 pad_maximum_fusion.2
  19.8 0.0 copy-start.8
  19.9 0.1 pad_maximum_fusion
  20.0 0.3 copy.44
  20.4 0.1 reshape.64.x_ref
  20.5 0.3 copy-done.2
  20.8 0.1 copy-done.3
  20.9 0.1 copy-done.4
  21.0 0.0 copy-done.5
  21.0 0.1 copy-done.8
  21.0 44.5 %block.1 = (bf16[4,48,384]{2,1,0:T(8,128)(2,1)S(1)}, bf16[576,192]{1,0:T(8,128)(2,1)S(1)}, bf16[6400,128]{1,0:T(8,128)(2,1)S(1)}) custom-call(bf16[576,192]{1,0:T(8,128)(2,1)S(1)} %reshape.64.x_ref, bf16[4,48,384]{2,1,0:T(8,128)(2,1)S(1)} %pad.17.ct_ref, f32[2,3456,128]{2,1,0:T(8,128)} %copy-done.9, s32[4,144,1]{2,1,0:T(8,128)S(1)} %broadcast_in_dim_reshape.4.regq_ref, ...), custom_call_target="tpu_custom_call" | custom-call | flops 20000000000 | bytes 8388608 | tf_op jit(solution)/shard_map/block/pallas_call | solution.py:386
  65.5 1.2 copy-done.10
  66.8 0.1 copy.54
  66.9 0.7 fusion.2
  67.6 4.4 %collective-permute-start.2 = (bf16[2,12,3,384]{3,0,2,1:T(2,128)(2,1)}, bf16[2,12,3,384]{3,0,2,1:T(2,128)(2,1)}, u32[]{:S(2)}, u32[]{:S(2)}) collective-permute-start(bf16[2,12,3,384]{3,0,2,1:T(2,128)(2,1)} %get-tuple-element.56), channel_id=1, source_target_pairs={{0,1},{1,2},{2,3},{3,4},{4,5},{5,6},{6,7},{7,8},{8,9},{9,10},{10,1... | collective-permute-start | bytes 165896 | tf_op jit(solution)/shard_map/ppermute | solution.py:331
  72.0 0.1 reshape.74
  72.1 0.3 copy.55
  72.5 0.9 fusion
  73.3 1.4 %copy-done.11 = bf16[6400,128]{1,0:T(8,128)(2,1)S(1)} copy-done((bf16[6400,128]{1,0:T(8,128)(2,1)S(1)}, bf16[6400,128]{1,0:T(8,128)(2,1)}, u32[]{:S(2)}) %copy-start.11) | copy-done | bytes 1638424
  74.8 46.4 %weight_sums.1 = (f32[192,576]{1,0:T(8,128)S(1)}, f32[192,192]{1,0:T(8,128)S(1)}, f32[192,768]{1,0:T(8,128)S(1)}, f32[768,192]{1,0:T(8,128)S(1)}, f32[768,384]{1,0:T(8,128)S(1)}, /*index=5*/f32[24,3328]{1,0:T(8,128)S(1)}) custom-call(bf16[6400,128]{1,0:T(8,128)(2,1)S(1)} %copy-done.11), custom_call_target="tpu_custom_call" | custom-call | flops 10000000000 | bytes 16777216 | tf_op jit(solution)/shard_map/weight_sums/pallas_call | solution.py:432
  121.2 0.7 copy-done
  121.9 0.8 reshape.76
  122.7 1.9 %copy.58 = f32[4,6,3312]{2,0,1:T(4,128)} copy(f32[4,6,3312]{2,1,0:T(8,128)} %reshape.76) | data formatting | bytes 635904
  124.5 1.1 copy.57
  125.6 1.6 %pad_maximum_fusion.3 = bf16[2,12,6,384]{3,0,2,1:T(2,128)(2,1)} fusion(bf16[2,12,3,384]{3,0,2,1:T(2,128)(2,1)S(1)} %copy-done.13, bf16[2,12,3,384]{3,0,2,1:T(2,128)(2,1)} %collective-permute-done.2), kind=kLoop, calls=%fused_computation.5 | loop fusion | flops 55296 | bytes 221184 | tf_op jit(solution)/shard_map/concatenate | solution.py:428
  127.2 1.3 %pad_maximum_fusion.1 = bf16[2,24,12,192]{3,0,2,1:T(2,128)(2,1)S(1)} fusion(bf16[2,24,6,192]{3,0,2,1:T(2,128)(2,1)S(1)} %get-tuple-element.51, bf16[2,24,6,192]{3,0,2,1:T(2,128)(2,1)} %collective-permute-done.3), kind=kLoop, calls=%fused_computation.1 | loop fusion | flops 110592 | bytes 442368 | tf_op jit(solution)/shard_map/concatenate | solution.py:429
  128.6 0.8 copy.56
  129.3 0.8 copy.63
  130.1 0.7 copy.64
  130.8 0.8 copy.65
  131.6 1.0 copy.66
  (41 shorter events, 0.4 us)
Async XLA Ops:
  0.6 4.2 %copy-start.14 = (s32[144,144]{1,0:T(8,128)S(1)}, s32[144,144]{1,0:T(8,128)}, u32[]{:S(2)}) copy-start(s32[144,144]{1,0:T(8,128)} %param.19) | copy-start | bytes 248836
  1.6 18.0 %collective-permute-start.1 = (bf16[2,12,3,384]{3,0,2,1:T(2,128)(2,1)S(1)}, bf16[2,12,3,384]{3,0,2,1:T(2,128)(2,1)S(1)}, u32[]{:S(2)}, u32[]{:S(2)}) collective-permute-start(bf16[2,12,3,384]{3,0,2,1:T(2,128)(2,1)S(1)} %get-tuple-element.59), channel_id=1, source_target_pairs={{0,15},{1,0},{2,1},{3,2},{4,3},{5,4},{6,5},{7,6},{8,7},{9,8},{10,9... | collective-permute-start | bytes 165896 | tf_op jit(solution)/shard_map/ppermute | solution.py:331
  3.3 16.6 %collective-permute-start = (bf16[2,24,6,192]{3,1,2,0:T(8,128)(2,1)S(1)}, bf16[2,24,6,192]{3,1,2,0:T(8,128)(2,1)S(1)}, u32[]{:S(2)}, u32[]{:S(2)}) collective-permute-start(bf16[2,24,6,192]{3,1,2,0:T(8,128)(2,1)S(1)} %get-tuple-element.53), channel_id=1, source_target_pairs={{0,15},{1,0},{2,1},{3,2},{4,3},{5,4},{6,5},{7,6},{8,7},{9,8},{10,9... | collective-permute-start | bytes 331784 | tf_op jit(solution)/shard_map/ppermute | solution.py:331
  4.8 13.9 %copy-start.16 = (s32[2,24]{1,0:T(2,128)S(1)}, s32[2,24]{1,0:T(2,128)}, u32[]{:S(2)}) copy-start(s32[2,24]{1,0:T(2,128)} %param.20) | copy-start | bytes 580
  4.9 14.4 %copy-start.15 = (f32[768]{0:T(1024)S(1)}, f32[768]{0:T(1024)}, u32[]{:S(2)}) copy-start(f32[768]{0:T(1024)} %param.24) | copy-start | bytes 9220
  4.9 14.5 %copy-start.12 = (bf16[768,192]{0,1:T(8,128)(2,1)S(1)}, bf16[768,192]{0,1:T(8,128)(2,1)}, u32[]{:S(2)}) copy-start(bf16[768,192]{0,1:T(8,128)(2,1)} %param.23) | copy-start | bytes 884740
  17.1 1.7 %copy-start.9 = (f32[2,3456,128]{2,1,0:T(8,128)}, f32[2,3456,128]{2,1,0:T(8,128)S(1)}, u32[]{:S(2)}) copy-start(f32[2,3456,128]{2,1,0:T(8,128)S(1)} %bias_rows.1.bias_ref) | copy-start | bytes 10616836
  19.7 1.1 copy-start.2
  19.8 1.1 copy-start.3
  19.8 1.2 copy-start.4
  19.8 1.2 copy-start.5
  19.8 1.2 copy-start.6
  19.8 1.2 copy-start.7
  19.8 1.2 copy-start.8
  65.5 1.2 copy-start.10
  67.6 58.0 %collective-permute-start.2 = (bf16[2,12,3,384]{3,0,2,1:T(2,128)(2,1)}, bf16[2,12,3,384]{3,0,2,1:T(2,128)(2,1)}, u32[]{:S(2)}, u32[]{:S(2)}) collective-permute-start(bf16[2,12,3,384]{3,0,2,1:T(2,128)(2,1)} %get-tuple-element.56), channel_id=1, source_target_pairs={{0,1},{1,2},{2,3},{3,4},{4,5},{5,6},{6,7},{7,8},{8,9},{9,10},{10,1... | collective-permute-start | bytes 165896 | tf_op jit(solution)/shard_map/ppermute | solution.py:331
  73.3 53.9 %collective-permute-start.3 = (bf16[2,24,6,192]{3,0,2,1:T(2,128)(2,1)}, bf16[2,24,6,192]{3,0,2,1:T(2,128)(2,1)}, u32[]{:S(2)}, u32[]{:S(2)}) collective-permute-start(bf16[2,24,6,192]{3,0,2,1:T(2,128)(2,1)} %get-tuple-element.50), channel_id=1, source_target_pairs={{0,1},{1,2},{2,3},{3,4},{4,5},{5,6},{6,7},{7,8},{8,9},{9,10},{10,1... | collective-permute-start | bytes 331784 | tf_op jit(solution)/shard_map/ppermute | solution.py:331
  73.3 1.4 %copy-start.11 = (bf16[6400,128]{1,0:T(8,128)(2,1)S(1)}, bf16[6400,128]{1,0:T(8,128)(2,1)}, u32[]{:S(2)}) copy-start(bf16[6400,128]{1,0:T(8,128)(2,1)} %copy-done.10) | copy-start | bytes 4915204
  121.2 0.7 copy-start
  122.7 2.9 %copy-start.13 = (bf16[2,12,3,384]{3,0,2,1:T(2,128)(2,1)S(1)}, bf16[2,12,3,384]{3,0,2,1:T(2,128)(2,1)}, u32[]{:S(2)}) copy-start(bf16[2,12,3,384]{3,0,2,1:T(2,128)(2,1)} %get-tuple-element.57) | copy-start | bytes 165892
  124.5 5.6 %copy-start.1 = (f32[192,192]{1,0:T(8,128)S(1)}, f32[192,192]{1,0:T(8,128)}, u32[]{:S(2)}) copy-start(f32[192,192]{1,0:T(8,128)} %copy-done) | copy-start | bytes 442372
